TPU v7x, 128 devices: a whole 4x4x4 slice. The times are simulated.
128 devices in a mesh: grp: 4 (over x), tile: 32 (over y, z, core).
Axes of the slice: x: 4, y: 4, z: 4, core: 2. Of those that a mesh axis runs over, the one named last changes fastest.
Arguments:
- descriptors: bfloat16 [64, 4096, 256], P('grp', 'tile'), may hold values from -8 to 8
- pairs: int32 [32, 2], P('grp'), may hold values from 0 to 63, as said below
- counts: int32 [64], replicated, may hold values from 1024 to 4096
Outputs:
- row_lse: float32 [32, 4096], P('grp', 'tile')
- col_lse: float32 [32, 4096], P('grp', 'tile')
- best_log: float32 [32, 4096], P('grp', 'tile')
Inputs may be any that keep to these rules, and one draw needn't show every extreme that they name: `pairs`: the two images of a pair differ.
All inputs are finite; a program needn't handle non-finite values.
Results may differ from a plain program's by a relative error of at most 0.0003.
Values may be sent and summed in bfloat16 or wider, within the bound.
A program may use at most 64 MiB of HBM per device.

v0:
```python
import math
import jax
import jax.numpy as jnp
from jax import lax
from jax.sharding import Mesh
from jax.sharding import PartitionSpec as P

QBLK = 4
TILE = ("tile_0", "tile_1", "tile_2")
NEGATIVE = -1e30


def in_one_piece(arrays, axis, split_dim, concat_dim, along):
    both = jnp.concatenate(arrays, axis=along)
    out, at, outs = (
        lax.all_to_all(both, axis, split_axis=split_dim, concat_axis=concat_dim, tiled=True),
        0,
        [],
    )
    for a in arrays:
        outs.append(lax.slice_in_dim(out, at, at + a.shape[along], axis=along))
        at += a.shape[along]
    return tuple(outs)


def in_blocks(value, dim, count):
    lengths = value.shape
    tiles = value.reshape(*lengths[:dim], count, lengths[dim] // count, *lengths[dim + 1 :])
    return jnp.moveaxis(tiles, dim, 0)


def joined_along(tiles, dim):
    lengths = list(tiles.shape[1:])
    lengths[dim] *= tiles.shape[0]
    return jnp.moveaxis(tiles, 0, dim).reshape(lengths)


def exchange_in_order(tiles, axes, turns):
    inside = tiles.shape[1:]
    out = tiles.reshape(*(lax.axis_size(a) for a in axes), *inside)
    for k in turns:
        out = lax.all_to_all(out, axes[k], k, k, tiled=True)
    return out.reshape(-1, *inside)


def core_and_chips(value, groups, turns, split_dim, concat_dim):
    count = lax.axis_size(groups[0]) * lax.axis_size(groups[1])
    tiles = in_blocks(value, split_dim, count)
    return joined_along(exchange_in_order(tiles, groups, turns), concat_dim)


def join_stats(earlier, later):
    highest = jnp.maximum(earlier[0], later[0])
    summed = earlier[1] * jnp.exp(earlier[0] - highest) + later[1] * jnp.exp(later[0] - highest)
    return (highest, summed)


def slot_first(item, query_index, score_scale):
    query_rows, key_image, query_count, key_count = item
    height = query_rows.shape[0]
    width = query_rows.shape[1]
    total_keys = key_image.shape[0]
    block = min(512, height)
    number = height // block
    key_mask = (lax.iota(jnp.int32, total_keys) < key_count)[None, :]
    grouped = query_rows.reshape(number, block, width)
    index_groups = query_index.reshape(number, block)

    def first_pass(carried, inputs):
        block_rows, block_index = inputs
        scores = (
            jnp.einsum("qd,kd->qk", block_rows, key_image, preferred_element_type=jnp.float32)
            * score_scale
        )
        query_mask = (block_index < query_count)[:, None]
        row_top = jnp.max(jnp.where(key_mask, scores, NEGATIVE), axis=1)
        row_total = jnp.sum(jnp.where(key_mask, jnp.exp(scores - row_top[:, None]), 0.0), axis=1)
        col_top = jnp.max(jnp.where(query_mask, scores, NEGATIVE), axis=0)
        col_total = jnp.sum(jnp.where(query_mask, jnp.exp(scores - col_top[None, :]), 0.0), axis=0)
        return (join_stats(carried, (col_top, col_total)), row_top + jnp.log(row_total))

    start_stats = (
        jnp.full((total_keys,), NEGATIVE, jnp.float32),
        jnp.zeros((total_keys,), jnp.float32),
    )
    col_stats, row_values = lax.scan(first_pass, start_stats, (grouped, index_groups))
    return (col_stats[0], col_stats[1], row_values.reshape(height))


def slot_second(item, query_index, score_scale):
    query_rows, key_image, row_values, col_values, query_count, key_count = item
    height = query_rows.shape[0]
    width = query_rows.shape[1]
    total_keys = key_image.shape[0]
    block = min(512, height)
    number = height // block
    key_mask = (lax.iota(jnp.int32, total_keys) < key_count)[None, :]
    grouped = query_rows.reshape(number, block, width)
    lse_groups = row_values.reshape(number, block)

    def second_pass(carried, inputs):
        block_rows, block_lse = inputs
        scores = (
            jnp.einsum("qd,kd->qk", block_rows, key_image, preferred_element_type=jnp.float32)
            * score_scale
        )
        best = (
            jnp.max(jnp.where(key_mask, 2.0 * scores - col_values[None, :], NEGATIVE), axis=1)
            - block_lse
        )
        return (carried, best)

    unused, best_values = lax.scan(second_pass, jnp.int32(0), (grouped, lse_groups))
    query_valid = query_index < query_count
    return (
        jnp.where(query_valid, row_values, 0.0),
        jnp.where(query_valid, best_values.reshape(height), 0.0),
    )


def paired_blocks(queries, keys_local, query_counts, key_counts, score_scale):
    devices_here = lax.axis_size(TILE)
    rows = queries.shape[1]
    width = queries.shape[2]
    slots = devices_here // QBLK
    sub = rows // QBLK
    pair_count = queries.shape[0]
    per_slot = -(-pair_count // slots)
    padded = per_slot * slots
    query_send = (
        queries.reshape(slots, per_slot, QBLK, sub, width)
        .transpose(0, 2, 1, 3, 4)
        .reshape(devices_here, per_slot, sub, width)
    )
    key_send = jnp.broadcast_to(
        keys_local.reshape(slots, 1, per_slot, rows, width), (slots, QBLK, per_slot, rows, width)
    ).reshape(devices_here, per_slot, rows, width)
    query_got, key_got = in_one_piece((query_send, key_send), TILE, 0, 0, 2)
    query_here = query_got.transpose(1, 0, 2, 3).reshape(per_slot, devices_here * sub, width)
    key_here = key_got.transpose(1, 0, 2, 3).reshape(per_slot, devices_here * rows, width)
    place = lax.axis_index(TILE)
    slot = place // QBLK
    quarter = place % QBLK
    query_index = (
        lax.iota(jnp.int32, devices_here)[:, None] * rows
        + quarter * sub
        + lax.iota(jnp.int32, sub)[None, :]
    ).reshape(devices_here * sub)
    query_own = lax.dynamic_slice_in_dim(query_counts, slot * per_slot, per_slot, 0)
    key_own = lax.dynamic_slice_in_dim(key_counts, slot * per_slot, per_slot, 0)
    col_top, col_total, row_values = lax.map(
        lambda item: slot_first(item, query_index, score_scale),
        (query_here, key_here, query_own, key_own),
    )

    def by_block(values):
        return values.reshape(per_slot, devices_here, rows).transpose(1, 0, 2)

    top_got, total_got = in_one_piece((by_block(col_top), by_block(col_total)), TILE, 0, 0, 1)
    top_got = top_got.reshape(slots, QBLK, per_slot, rows)
    total_got = total_got.reshape(slots, QBLK, per_slot, rows)
    stats = (top_got[:, 0], total_got[:, 0])
    for member in range(1, QBLK):
        stats = join_stats(stats, (top_got[:, member], total_got[:, member]))
    col_block = stats[0] + jnp.log(stats[1])
    col_send = jnp.broadcast_to(col_block[:, None], (slots, QBLK, per_slot, rows)).reshape(
        devices_here, per_slot, rows
    )
    col_got = core_and_chips(col_send, (("tile_0", "tile_1"), "tile_2"), (1, 0), 0, 0)
    col_values = col_got.transpose(1, 0, 2).reshape(per_slot, devices_here * rows)
    row_out, best_out = lax.map(
        lambda item: slot_second(item, query_index, score_scale),
        (query_here, key_here, row_values, col_values, query_own, key_own),
    )

    def to_owner(values):
        return values.reshape(per_slot, devices_here, sub).transpose(1, 0, 2)

    row_got, best_got = (
        lax.all_to_all(to_owner(row_out), TILE, split_axis=0, concat_axis=0, tiled=True),
        lax.all_to_all(to_owner(best_out), TILE, split_axis=0, concat_axis=0, tiled=True),
    )

    def from_slots(values):
        return (
            values.reshape(slots, QBLK, per_slot, sub).transpose(0, 2, 1, 3).reshape(padded, rows)
        )

    key_place = place * rows + lax.iota(jnp.int32, rows)
    key_valid_own = key_place[None, :] < key_counts[:, None]
    col_out = jnp.where(key_valid_own, col_block.reshape(padded, rows), 0.0)
    return (from_slots(row_got), col_out, from_slots(best_got))


def local(descriptors, pairs, counts):
    score_scale = 2.0 / math.sqrt(descriptors.shape[2])
    image_rows = lax.all_gather(descriptors, "grp", axis=0, tiled=True)
    image_ids = lax.iota(jnp.int32, counts.shape[0])
    first_image = pairs[:, 0]
    second = pairs[:, 1]
    query_counts = jnp.sum(
        jnp.where(first_image[:, None] == image_ids[None, :], counts[None, :], 0), axis=1
    )
    key_counts = jnp.sum(
        jnp.where(second[:, None] == image_ids[None, :], counts[None, :], 0), axis=1
    )
    queries = jnp.take(image_rows, first_image, axis=0)
    keys_local = jnp.take(image_rows, second, axis=0)
    return paired_blocks(queries, keys_local, query_counts, key_counts, score_scale)


def solution(mesh):
    torus = Mesh(
        mesh.devices.reshape(mesh.shape["grp"], 4, 4, 2), ("grp", "tile_0", "tile_1", "tile_2")
    )
    return jax.shard_map(
        local,
        mesh=torus,
        in_specs=(P("grp", TILE, None), P("grp", None), P()),
        out_specs=(P("grp", TILE), P("grp", TILE), P("grp", TILE)),
        check_vma=False,
    )
```

profile of v0, /device:TPU:1, one launch (start us, length us, event | category | flops | bytes accessed | tf_op | source)
XLA Modules:
  0.0 198.5 jit_solution(10425971025592148428)
XLA Ops:
  7.2 0.0 all-gather.2.cloned.1.call-start
  7.2 0.7 all-gather.2.cloned.1.call-update
  7.9 0.8 compare_and_fusion.1
  8.7 52.2 %all-gather.2.cloned.1.call-done = bf16[64,128,256]{2,1,0:T(8,128)(2,1)} async-done(((bf16[16,128,256]{2,1,0:T(8,128)(2,1)}), bf16[64,128,256]{2,1,0:T(8,128)(2,1)}) %all-gather.2.cloned.1.call-update) | async-done | bytes 4194320 | tf_op jit(solution)/shard_map/all_gather | solution.py:197
  60.9 2.8 %gather_fusion = bf16[8,128,256]{2,1,0:T(8,128)(2,1)S(1)} fusion(bf16[64,128,256]{2,1,0:T(8,128)(2,1)} %all-gather.2.cloned.1.call-done, s32[1024]{0:T(1024)S(1)} %pad_clamp_fusion.1), kind=kCustom, calls=%fused_computation.clone | custom fusion | bytes 1048608 | tf_op jit(solution)/shard_map/jit(_take)/gather | solution.py:207
  63.6 0.0 copy-start
  63.7 0.0 copy-start.1
  63.7 2.8 %gather_fusion.1 = bf16[8,128,256]{2,1,0:T(8,128)(2,1)S(1)} fusion(bf16[64,128,256]{2,1,0:T(8,128)(2,1)} %all-gather.2.cloned.1.call-done, s32[1024]{0:T(1024)S(1)} %pad_clamp_fusion), kind=kCustom, calls=%fused_computation.1.clone | custom fusion | bytes 1048608 | tf_op jit(solution)/shard_map/jit(_take)/gather | solution.py:208
  66.5 0.2 broadcast_select_fusion
  66.6 0.2 broadcast_in_dim.140
  66.9 1.7 pad_maximum_fusion
  68.6 7.9 %all-to-all-start = ((bf16[32,1,160,256]{3,2,1,0:T(8,128)(2,1)}), bf16[32,1,160,256]{3,2,1,0:T(8,128)(2,1)S(1)}, u32[]{:S(2)}, u32[]{:S(2)}) async-start(bf16[32,1,160,256]{3,2,1,0:T(8,128)(2,1)} %pad_maximum_fusion), calls=%async_computation | async-start | bytes 5242880 | tf_op jit(solution)/shard_map/all_to_all | solution.py:16
  76.5 0.0 copy-done
  76.5 0.0 copy-done.1
  76.5 0.2 select_reduce_fusion.5
  76.8 0.6 dynamic_slice.52
  77.4 0.6 dynamic_slice.53
  77.9 0.1 add.159
  78.0 0.1 add.160
  78.1 0.1 add.162
  78.2 32.2 %all-to-all-done = bf16[32,1,160,256]{3,2,1,0:T(8,128)(2,1)S(1)} async-done(((bf16[32,1,160,256]{3,2,1,0:T(8,128)(2,1)}), bf16[32,1,160,256]{3,2,1,0:T(8,128)(2,1)S(1)}, u32[]{:S(2)}, u32[]{:S(2)}) %all-to-all-start) | async-done | bytes 2621472 | tf_op jit(solution)/shard_map/all_to_all | solution.py:16
  110.4 1.5 slice.61
  112.0 20.6 %while.48 = (s32[]{:T(128)}, f32[4096]{0:T(1024)S(1)}, f32[4096]{0:T(1024)S(1)}, f32[2,512]{1,0:T(2,128)S(1)}, s32[2,512]{1,0:T(2,128)S(1)}, /*index=5*/s32[]{:T...) while((s32[]{:T(128)}, f32[4096]{0:T(1024)S(1)}, ...), condition=%wide.region_7.9_spmd.clone, body=%wide.region_2.8_spmd.clone.sunk | while | flops 1098936320 | bytes 19316360 | solution.py:86
  112.0 0.7 compare_reduce_fusion.8
  112.6 0.7 compare_reduce_fusion.7
  113.3 4.0 %select_reduce_fusion.11 = (f32[512]{0:T(512)S(1)}, f32[4096]{0:T(1024)S(1)}, f32[512,4096]{1,0:T(8,128)S(1)}) fusion(pred[4096]{0:T(1024)(128)(4,1)S(1)} %compare_reduce_fusion.7, pred[512]{0:T(512)(128)(4,1)S(1)} %compare_reduce_fusion.8, bf16[4096,256]{1,0:T(8,128)(2,1)} %get-tuple-element.457, bf16[2,512,256]{2,1,0:T(8,128)(2,1)S(1)} %get-tuple-element.456, ...), kind=kOutput, calls=%fused_computation.11.clone.1 | convolution fusion | flops 1084222976 | bytes 10770948 | tf_op jit(solution)/shard_map/while/body/eval_jaxpr/while/body/eval_jaxpr/qd,kd->qk/dot_general | solution.py:72
  117.3 4.8 %select_reduce_fusion.12 = (f32[512]{0:T(512)S(1)}, f32[4096]{0:T(1024)S(1)}) fusion(f32[512,4096]{1,0:T(8,128)S(1)} %get-tuple-element.421, f32[512]{0:T(512)S(1)} %get-tuple-element.422, pred[4096]{0:T(1024)(128)(4,1)S(1)} %compare_reduce_fusion.7, f32[4096]{0:T(1024)S(1)} %get-tuple-element.423, pred[512]{0:T(512)(128)(4,1)S(1)} %compare_reduce_fusion.8), kind=kLoop, calls=%fused_computation.10.clone.1 | loop fusion | flops 14675456 | bytes 8430080 | tf_op jit(solution)/shard_map/while/body/eval_jaxpr/while/body/eval_jaxpr/reduce_sum | solution.py:77
  122.3 0.7 compare_reduce_fusion.8
  122.9 0.7 compare_reduce_fusion.7
  123.6 3.9 %select_reduce_fusion.11 = (f32[512]{0:T(512)S(1)}, f32[4096]{0:T(1024)S(1)}, f32[512,4096]{1,0:T(8,128)S(1)}) fusion(pred[4096]{0:T(1024)(128)(4,1)S(1)} %compare_reduce_fusion.7, pred[512]{0:T(512)(128)(4,1)S(1)} %compare_reduce_fusion.8, bf16[4096,256]{1,0:T(8,128)(2,1)} %get-tuple-element.457, bf16[2,512,256]{2,1,0:T(8,128)(2,1)S(1)} %get-tuple-element.456, ...), kind=kOutput, calls=%fused_computation.11.clone.1 | convolution fusion | flops 1084222976 | bytes 10770948 | tf_op jit(solution)/shard_map/while/body/eval_jaxpr/while/body/eval_jaxpr/qd,kd->qk/dot_general | solution.py:72
  127.6 4.8 %select_reduce_fusion.12 = (f32[512]{0:T(512)S(1)}, f32[4096]{0:T(1024)S(1)}) fusion(f32[512,4096]{1,0:T(8,128)S(1)} %get-tuple-element.421, f32[512]{0:T(512)S(1)} %get-tuple-element.422, pred[4096]{0:T(1024)(128)(4,1)S(1)} %compare_reduce_fusion.7, f32[4096]{0:T(1024)S(1)} %get-tuple-element.423, pred[512]{0:T(512)(128)(4,1)S(1)} %compare_reduce_fusion.8), kind=kLoop, calls=%fused_computation.10.clone.1 | loop fusion | flops 14675456 | bytes 8430080 | tf_op jit(solution)/shard_map/while/body/eval_jaxpr/while/body/eval_jaxpr/reduce_sum | solution.py:77
  132.6 11.1 %all_to_all.30 = f32[32,2,128]{2,1,0:T(2,128)S(1)} all-to-all(f32[32,2,128]{2,1,0:T(2,128)S(1)} %pad_maximum_fusion.1), channel_id=1, replica_groups=mesh['grp'=4,'tile_0'=4,'tile_1'=4,'tile_2'=2] {'tile_0','tile_1','tile_2'}, dimensions={0} | all-to-all | bytes 65536 | tf_op jit(solution)/shard_map/all_to_all | solution.py:16
  143.8 3.8 %all_to_all.31 = f32[16,2,1,1,128]{4,3,2,0,1:T(1,128)S(1)} all-to-all(f32[16,2,1,1,128]{4,3,2,0,1:T(1,128)S(1)} %broadcast_in_dim.147), channel_id=1, replica_groups=mesh['grp'=4,'tile_0'=4,'tile_1'=4,'tile_2'=2] {'tile_2'}, dimensions={1} | all-to-all | bytes 32768 | tf_op jit(solution)/shard_map/all_to_all | solution.py:42
  147.5 0.6 copy.107
  148.1 3.5 %all-to-all-start.4 = ((f32[16,2,1,1,128]{4,3,2,1,0:T(1,128)}), f32[16,2,1,1,128]{4,3,2,1,0:T(1,128)S(1)}, u32[]{:S(2)}, u32[]{:S(2)}) async-start(f32[16,2,1,1,128]{4,3,2,1,0:T(1,128)} %copy.107), calls=%async_computation.4 | async-start | bytes 32768 | tf_op jit(solution)/shard_map/all_to_all | solution.py:42
  151.7 0.1 squeeze.81
  151.8 6.3 %all-to-all-done.4 = f32[16,2,1,1,128]{4,3,2,1,0:T(1,128)S(1)} async-done(((f32[16,2,1,1,128]{4,3,2,1,0:T(1,128)}), f32[16,2,1,1,128]{4,3,2,1,0:T(1,128)S(1)}, u32[]{:S(2)}, u32[]{:S(2)}) %all-to-all-start.4) | async-done | bytes 16416 | tf_op jit(solution)/shard_map/all_to_all | solution.py:42
  158.0 7.6 %while.47 = (s32[]{:T(128)}, f32[2,512]{1,0:T(2,128)S(1)}, bf16[2,512,256]{2,1,0:T(8,128)(2,1)S(1)}, bf16[4096,256]{1,0:T(8,128)(2,1)}, f32[4096]{0:T(1024)S(1)}...) while((s32[]{:T(128)}, f32[2,512]{1,0:T(2,128)S(1)}, ...), condition=%wide.region_10.12_spmd.clone, body=%wide.region_8.11_spmd.clone.sunk | while | flops 1082134528 | bytes 2396269 | solution.py:113
  158.0 0.7 compare_reduce_fusion.6
  158.7 3.0 %select_reduce_fusion.10 = f32[512]{0:T(512)S(1)} fusion(bf16[4096,256]{1,0:T(8,128)(2,1)} %get-tuple-element.482, f32[4096]{0:T(1024)S(1)} %get-tuple-element.483, pred[4096]{0:T(1024)(128)(4,1)S(1)} %compare_reduce_fusion.6, bf16[2,512,256]{2,1,0:T(8,128)(2,1)S(1)} %get-tuple-element.481, s32[]{:T(128)} %get-tuple-element.470), kind=kOutput, calls=%fused_computation.4.clone.1 | convolution fusion | flops 1082129920 | bytes 2381828 | tf_op jit(solution)/shard_map/while/body/eval_jaxpr/while/body/eval_jaxpr/qd,kd->qk/dot_general | solution.py:104
  161.8 0.7 compare_reduce_fusion.6
  162.5 3.0 %select_reduce_fusion.10 = f32[512]{0:T(512)S(1)} fusion(bf16[4096,256]{1,0:T(8,128)(2,1)} %get-tuple-element.482, f32[4096]{0:T(1024)S(1)} %get-tuple-element.483, pred[4096]{0:T(1024)(128)(4,1)S(1)} %compare_reduce_fusion.6, bf16[2,512,256]{2,1,0:T(8,128)(2,1)S(1)} %get-tuple-element.481, s32[]{:T(128)} %get-tuple-element.470), kind=kOutput, calls=%fused_computation.4.clone.1 | convolution fusion | flops 1082129920 | bytes 2381828 | tf_op jit(solution)/shard_map/while/body/eval_jaxpr/while/body/eval_jaxpr/qd,kd->qk/dot_general | solution.py:104
  165.6 0.1 reshape.246
  165.7 1.4 compare_select_fusion
  167.1 4.9 %all-to-all-start.1 = ((f32[32,1,32]{2,1,0:T(1,128)}), f32[32,1,32]{2,1,0:T(1,128)S(1)}, u32[]{:S(2)}, u32[]{:S(2)}) async-start(f32[32,1,32]{2,1,0:T(1,128)} %get-tuple-element.313), calls=%async_computation.1 | async-start | bytes 32768 | tf_op jit(solution)/shard_map/all_to_all | solution.py:180
  172.0 7.1 %all-to-all-done.1 = f32[32,1,32]{2,1,0:T(1,128)S(1)} async-done(((f32[32,1,32]{2,1,0:T(1,128)}), f32[32,1,32]{2,1,0:T(1,128)S(1)}, u32[]{:S(2)}, u32[]{:S(2)}) %all-to-all-start.1) | async-done | bytes 4128 | tf_op jit(solution)/shard_map/all_to_all | solution.py:180
  179.1 4.2 %all-to-all-start.5 = ((f32[32,1,32]{2,1,0:T(1,128)}), f32[32,1,32]{2,1,0:T(1,128)S(1)}, u32[]{:S(2)}, u32[]{:S(2)}) async-start(f32[32,1,32]{2,1,0:T(1,128)} %get-tuple-element.312), calls=%async_computation.5 | async-start | bytes 32768 | tf_op jit(solution)/shard_map/all_to_all | solution.py:181
  183.2 0.7 add_select_fusion
  183.9 0.5 broadcast.199
  184.4 0.7 reduce.12
  185.1 0.7 reshape_transpose_reshape.10
  185.8 4.5 %all-to-all-done.5 = f32[32,1,32]{2,1,0:T(1,128)S(1)} async-done(((f32[32,1,32]{2,1,0:T(1,128)}), f32[32,1,32]{2,1,0:T(1,128)S(1)}, u32[]{:S(2)}, u32[]{:S(2)}) %all-to-all-start.5) | async-done | bytes 4128 | tf_op jit(solution)/shard_map/all_to_all | solution.py:181
  190.3 0.7 reduce.13
  191.0 0.7 reshape_transpose_reshape.11
  (30 shorter events, 0.5 us)
Async XLA Ops:
  7.2 53.7 %all-gather.2.cloned.1.call-start = ((), (), s32[]{:S(2)}) async-start(), calls=%async_computation.6 | async-start | bytes 5242880 | tf_op jit(solution)/shard_map/all_gather | solution.py:197
  63.6 12.9 %copy-start = (s32[8,2]{0,1:T(2,128)S(1)}, s32[8,2]{0,1:T(2,128)}, u32[]{:S(2)}) copy-start(s32[8,2]{0,1:T(2,128)} %param.10) | copy-start | bytes 196
  63.7 12.9 %copy-start.1 = (s32[64]{0:T(128)S(1)}, s32[64]{0:T(128)}, u32[]{:S(2)}) copy-start(s32[64]{0:T(128)} %param.11) | copy-start | bytes 772
  68.6 41.8 %all-to-all-start = ((bf16[32,1,160,256]{3,2,1,0:T(8,128)(2,1)}), bf16[32,1,160,256]{3,2,1,0:T(8,128)(2,1)S(1)}, u32[]{:S(2)}, u32[]{:S(2)}) async-start(bf16[32,1,160,256]{3,2,1,0:T(8,128)(2,1)} %pad_maximum_fusion), calls=%async_computation | async-start | bytes 5242880 | tf_op jit(solution)/shard_map/all_to_all | solution.py:16
  148.1 9.9 %all-to-all-start.4 = ((f32[16,2,1,1,128]{4,3,2,1,0:T(1,128)}), f32[16,2,1,1,128]{4,3,2,1,0:T(1,128)S(1)}, u32[]{:S(2)}, u32[]{:S(2)}) async-start(f32[16,2,1,1,128]{4,3,2,1,0:T(1,128)} %copy.107), calls=%async_computation.4 | async-start | bytes 32768 | tf_op jit(solution)/shard_map/all_to_all | solution.py:42
  167.1 12.0 %all-to-all-start.1 = ((f32[32,1,32]{2,1,0:T(1,128)}), f32[32,1,32]{2,1,0:T(1,128)S(1)}, u32[]{:S(2)}, u32[]{:S(2)}) async-start(f32[32,1,32]{2,1,0:T(1,128)} %get-tuple-element.313), calls=%async_computation.1 | async-start | bytes 32768 | tf_op jit(solution)/shard_map/all_to_all | solution.py:180
  179.1 11.2 %all-to-all-start.5 = ((f32[32,1,32]{2,1,0:T(1,128)}), f32[32,1,32]{2,1,0:T(1,128)S(1)}, u32[]{:S(2)}, u32[]{:S(2)}) async-start(f32[32,1,32]{2,1,0:T(1,128)} %get-tuple-element.312), calls=%async_computation.5 | async-start | bytes 32768 | tf_op jit(solution)/shard_map/all_to_all | solution.py:181
Sparse Core Ops, SparseCore 0:
  9.6 51.1 all-gather.1
where the time goes:
time: 199 us
  waiting for transfers between devices  103 us (52%)
  starting transfers between devices  20.5 us (10%)
  other arithmetic  20.3 us (10%)
  blocking collectives  14.8 us (7%)
  between operations  14.3 us (7%)
  matrix products  13.9 us (7%)
  local copies, waits for them, and re-layouts  11.7 us (6%)
    all_gather x1, waiting for transfers between devices, local(): image_rows = lax.all_gather(descriptors, 'grp', axis=0, tiled=True)  52.2 us
    all_to_all x1, waiting for transfers between devices, in_one_piece(): lax.all_to_all(both, axis, split_axis=split_dim, concat_axis=concat_dim,...  32.2 us
    all_to_all x1, blocking collectives, in_one_piece(): lax.all_to_all(both, axis, split_axis=split_dim, concat_axis=concat_dim,...  11.1 us
    reduce_sum x2, other arithmetic, first_pass(): jnp.sum(jnp.where(key_mask, jnp.exp(scores - row_top[:, None]), 0.0), axi...  9.7 us
    dot_general x2, matrix products, first_pass(): jnp.einsum('qd,kd->qk', block_rows, key_image, preferred_element_type=jnp...  7.9 us
    all_to_all x1, starting transfers between devices, in_one_piece(): lax.all_to_all(both, axis, split_axis=split_dim, concat_axis=concat_dim,...  7.87 us
    all_to_all x1, waiting for transfers between devices, paired_blocks(): lax.all_to_all(to_owner(row_out), TILE, split_axis=0, concat_axis=0, tile...  7.06 us
    all_to_all x1, waiting for transfers between devices, exchange_in_order(): out = lax.all_to_all(out, axes[k], k, k, tiled=True)  6.28 us
  transfers between devices with their start and end apart: 5, of which 5 were waited for; matrix products, arithmetic and copies ran while one was open for 3% of the time, Pallas kernels for 0%

commit v1 on v0

--- a/solution.py
+++ b/solution.py
@@ -194,7 +194,8 @@
 
 def local(descriptors, pairs, counts):
     score_scale = 2.0 / math.sqrt(descriptors.shape[2])
-    image_rows = lax.all_gather(descriptors, "grp", axis=0, tiled=True)
+    sent = jnp.stack([descriptors] * lax.axis_size("grp"))
+    image_rows = jnp.concatenate(lax.all_to_all(sent, "grp", 0, 0), axis=0)
     image_ids = lax.iota(jnp.int32, counts.shape[0])
     first_image = pairs[:, 0]
     second = pairs[:, 1]

time: 199 us -> 191 us (0.960)
  between operations: 14.3 us -> 0.94 us
  starting transfers between devices: 20.5 us -> 27.4 us
  waiting for transfers between devices: 103 us -> 98.8 us
  local copies, waits for them, and re-layouts: 11.7 us -> 15.4 us
    all_gather x1 -> x0, waiting for transfers between devices: 52.2 us -> none  [local(): image_rows = lax.all_gather(descriptors, 'grp', axis=0, tiled=True)]
    all_to_all x0 -> x1, waiting for transfers between devices: none -> 48.7 us  [local(): image_rows = jnp.concatenate(lax.all_to_all(sent, 'grp', 0, 0), axis=0)]
    all_to_all x0 -> x1, starting transfers between devices: none -> 4.86 us  [local(): image_rows = jnp.concatenate(lax.all_to_all(sent, 'grp', 0, 0), axis=0)]
    another operation x2 -> x3, local copies, waits for them, and re-layouts: 0.01 us -> 3.72 us  [the longest x1 3.71 us: local(): sent = jnp.stack([descriptors] * lax.axis_size('grp'))]
    all_to_all x1, starting transfers between devices: 7.87 us -> 9.97 us  [in_one_piece(): lax.all_to_all(both, axis, split_axis=split_dim, concat_axis=concat_dim,...]
  transfers between devices with their start and end apart: 5 -> 5, of which waited for: 5 -> 5; matrix products, arithmetic and copies ran while one was open for 3% -> 2% of each run, Pallas kernels for 0% -> 0%
where the time goes in v1:
time: 191 us
  waiting for transfers between devices  98.8 us (52%)
  starting transfers between devices  27.4 us (14%)
  other arithmetic  19.5 us (10%)
  local copies, waits for them, and re-layouts  15.4 us (8%)
  blocking collectives  14.8 us (8%)
  matrix products  13.7 us (7%)
    all_to_all x1, waiting for transfers between devices, local(): image_rows = jnp.concatenate(lax.all_to_all(sent, 'grp', 0, 0), axis=0)  48.7 us
    all_to_all x1, waiting for transfers between devices, in_one_piece(): lax.all_to_all(both, axis, split_axis=split_dim, concat_axis=concat_dim,...  32.2 us
    all_to_all x1, blocking collectives, in_one_piece(): lax.all_to_all(both, axis, split_axis=split_dim, concat_axis=concat_dim,...  11.1 us
    all_to_all x1, starting transfers between devices, in_one_piece(): lax.all_to_all(both, axis, split_axis=split_dim, concat_axis=concat_dim,...  9.97 us
    reduce_sum x2, other arithmetic, first_pass(): jnp.sum(jnp.where(key_mask, jnp.exp(scores - row_top[:, None]), 0.0), axi...  9.69 us
    dot_general x2, matrix products, first_pass(): jnp.einsum('qd,kd->qk', block_rows, key_image, preferred_element_type=jnp...  7.68 us
    all_to_all x1, waiting for transfers between devices, paired_blocks(): lax.all_to_all(to_owner(row_out), TILE, split_axis=0, concat_axis=0, tile...  7.06 us
    all_to_all x1, waiting for transfers between devices, exchange_in_order(): out = lax.all_to_all(out, axes[k], k, k, tiled=True)  6.28 us
  transfers between devices with their start and end apart: 5, of which 5 were waited for; matrix products, arithmetic and copies ran while one was open for 2% of the time, Pallas kernels for 0%

profile of v1, /device:TPU:1, one launch (start us, length us, event | category | flops | bytes accessed | tf_op | source)
XLA Modules:
  0.0 190.6 jit_solution(13784941173569258639)
XLA Ops:
  0.6 0.0 copy-start
  0.6 3.7 %stack.2 = bf16[4,16,128,256]{3,2,1,0:T(8,128)(2,1)} broadcast(bf16[16,128,256]{2,1,0:T(8,128)(2,1)} %param.9), dimensions={1,2,3} | broadcast | bytes 5242880 | tf_op jit(solution)/shard_map/stack | solution.py:197
  4.4 4.9 %all-to-all-start = ((bf16[4,16,128,256]{3,2,1,0:T(8,128)(2,1)}), bf16[4,16,128,256]{3,2,1,0:T(8,128)(2,1)}, u32[]{:S(2)}, u32[]{:S(2)}) async-start(bf16[4,16,128,256]{3,2,1,0:T(8,128)(2,1)} %stack.2), calls=%async_computation | async-start | bytes 8388608 | tf_op jit(solution)/shard_map/all_to_all | solution.py:198
  9.2 0.0 copy-done
  9.3 48.7 %all-to-all-done = bf16[4,16,128,256]{3,2,1,0:T(8,128)(2,1)} async-done(((bf16[4,16,128,256]{3,2,1,0:T(8,128)(2,1)}), bf16[4,16,128,256]{3,2,1,0:T(8,128)(2,1)}, u32[]{:S(2)}, u32[]{:S(2)}) %all-to-all-start) | async-done | bytes 4194336 | tf_op jit(solution)/shard_map/all_to_all | solution.py:198
  58.0 2.8 %gather_fusion = bf16[8,128,256]{2,1,0:T(8,128)(2,1)S(1)} fusion(bf16[64,128,256]{2,1,0:T(8,128)(2,1)} %bitcast.2, s32[1024]{0:T(1024)S(1)} %pad_clamp_fusion.1), kind=kCustom, calls=%fused_computation.clone | custom fusion | bytes 1048608 | tf_op jit(solution)/shard_map/jit(_take)/gather | solution.py:208
  60.8 0.0 copy-start.1
  60.8 2.8 %gather_fusion.1 = bf16[8,128,256]{2,1,0:T(8,128)(2,1)S(1)} fusion(bf16[64,128,256]{2,1,0:T(8,128)(2,1)} %bitcast.2, s32[1024]{0:T(1024)S(1)} %pad_clamp_fusion), kind=kCustom, calls=%fused_computation.1.clone | custom fusion | bytes 1048608 | tf_op jit(solution)/shard_map/jit(_take)/gather | solution.py:209
  63.5 0.2 broadcast_select_fusion
  63.7 0.2 broadcast_in_dim.140
  64.0 1.7 pad_maximum_fusion
  65.7 10.0 %all-to-all-start.1 = ((bf16[32,1,160,256]{3,2,1,0:T(8,128)(2,1)}), bf16[32,1,160,256]{3,2,1,0:T(8,128)(2,1)S(1)}, u32[]{:S(2)}, u32[]{:S(2)}) async-start(bf16[32,1,160,256]{3,2,1,0:T(8,128)(2,1)} %pad_maximum_fusion), calls=%async_computation.1 | async-start | bytes 5242880 | tf_op jit(solution)/shard_map/all_to_all | solution.py:16
  75.7 0.0 copy-done.1
  75.7 0.2 select_reduce_fusion.5
  75.9 0.6 dynamic_slice.52
  76.5 0.6 dynamic_slice.53
  77.1 0.1 add.159
  77.2 0.1 add.160
  77.3 0.1 add.162
  77.4 32.2 %all-to-all-done.1 = bf16[32,1,160,256]{3,2,1,0:T(8,128)(2,1)S(1)} async-done(((bf16[32,1,160,256]{3,2,1,0:T(8,128)(2,1)}), bf16[32,1,160,256]{3,2,1,0:T(8,128)(2,1)S(1)}, u32[]{:S(2)}, u32[]{:S(2)}) %all-to-all-start.1) | async-done | bytes 2621472 | tf_op jit(solution)/shard_map/all_to_all | solution.py:16
  109.6 1.5 slice.61
  111.1 20.4 %while.48 = (s32[]{:T(128)}, f32[4096]{0:T(1024)S(1)}, f32[4096]{0:T(1024)S(1)}, f32[2,512]{1,0:T(2,128)S(1)}, s32[2,512]{1,0:T(2,128)S(1)}, /*index=5*/s32[]{:T...) while((s32[]{:T(128)}, f32[4096]{0:T(1024)S(1)}, ...), condition=%wide.region_7.9_spmd.clone, body=%wide.region_2.8_spmd.clone.sunk | while | flops 1098936320 | bytes 19316360 | solution.py:86
  111.2 0.7 compare_reduce_fusion.8
  111.8 0.7 compare_reduce_fusion.7
  112.5 3.8 %select_reduce_fusion.11 = (f32[512]{0:T(512)S(1)}, f32[4096]{0:T(1024)S(1)}, f32[512,4096]{1,0:T(8,128)S(1)}) fusion(pred[4096]{0:T(1024)(128)(4,1)S(1)} %compare_reduce_fusion.7, pred[512]{0:T(512)(128)(4,1)S(1)} %compare_reduce_fusion.8, bf16[4096,256]{1,0:T(8,128)(2,1)} %get-tuple-element.457, bf16[2,512,256]{2,1,0:T(8,128)(2,1)S(1)} %get-tuple-element.456, ...), kind=kOutput, calls=%fused_computation.11.clone.1 | convolution fusion | flops 1084222976 | bytes 10770948 | tf_op jit(solution)/shard_map/while/body/eval_jaxpr/while/body/eval_jaxpr/qd,kd->qk/dot_general | solution.py:72
  116.4 4.8 %select_reduce_fusion.12 = (f32[512]{0:T(512)S(1)}, f32[4096]{0:T(1024)S(1)}) fusion(f32[512,4096]{1,0:T(8,128)S(1)} %get-tuple-element.421, f32[512]{0:T(512)S(1)} %get-tuple-element.422, pred[4096]{0:T(1024)(128)(4,1)S(1)} %compare_reduce_fusion.7, f32[4096]{0:T(1024)S(1)} %get-tuple-element.423, pred[512]{0:T(512)(128)(4,1)S(1)} %compare_reduce_fusion.8), kind=kLoop, calls=%fused_computation.10.clone.1 | loop fusion | flops 14675456 | bytes 8430080 | tf_op jit(solution)/shard_map/while/body/eval_jaxpr/while/body/eval_jaxpr/reduce_sum | solution.py:77
  121.3 0.7 compare_reduce_fusion.8
  122.0 0.7 compare_reduce_fusion.7
  122.7 3.8 %select_reduce_fusion.11 = (f32[512]{0:T(512)S(1)}, f32[4096]{0:T(1024)S(1)}, f32[512,4096]{1,0:T(8,128)S(1)}) fusion(pred[4096]{0:T(1024)(128)(4,1)S(1)} %compare_reduce_fusion.7, pred[512]{0:T(512)(128)(4,1)S(1)} %compare_reduce_fusion.8, bf16[4096,256]{1,0:T(8,128)(2,1)} %get-tuple-element.457, bf16[2,512,256]{2,1,0:T(8,128)(2,1)S(1)} %get-tuple-element.456, ...), kind=kOutput, calls=%fused_computation.11.clone.1 | convolution fusion | flops 1084222976 | bytes 10770948 | tf_op jit(solution)/shard_map/while/body/eval_jaxpr/while/body/eval_jaxpr/qd,kd->qk/dot_general | solution.py:72
  126.6 4.8 %select_reduce_fusion.12 = (f32[512]{0:T(512)S(1)}, f32[4096]{0:T(1024)S(1)}) fusion(f32[512,4096]{1,0:T(8,128)S(1)} %get-tuple-element.421, f32[512]{0:T(512)S(1)} %get-tuple-element.422, pred[4096]{0:T(1024)(128)(4,1)S(1)} %compare_reduce_fusion.7, f32[4096]{0:T(1024)S(1)} %get-tuple-element.423, pred[512]{0:T(512)(128)(4,1)S(1)} %compare_reduce_fusion.8), kind=kLoop, calls=%fused_computation.10.clone.1 | loop fusion | flops 14675456 | bytes 8430080 | tf_op jit(solution)/shard_map/while/body/eval_jaxpr/while/body/eval_jaxpr/reduce_sum | solution.py:77
  131.5 11.1 %all_to_all.35 = f32[32,2,128]{2,1,0:T(2,128)S(1)} all-to-all(f32[32,2,128]{2,1,0:T(2,128)S(1)} %pad_maximum_fusion.1), channel_id=1, replica_groups=mesh['grp'=4,'tile_0'=4,'tile_1'=4,'tile_2'=2] {'tile_0','tile_1','tile_2'}, dimensions={0} | all-to-all | bytes 65536 | tf_op jit(solution)/shard_map/all_to_all | solution.py:16
  142.7 3.8 %all_to_all.36 = f32[16,2,1,1,128]{4,3,2,0,1:T(1,128)S(1)} all-to-all(f32[16,2,1,1,128]{4,3,2,0,1:T(1,128)S(1)} %broadcast_in_dim.147), channel_id=1, replica_groups=mesh['grp'=4,'tile_0'=4,'tile_1'=4,'tile_2'=2] {'tile_2'}, dimensions={1} | all-to-all | bytes 32768 | tf_op jit(solution)/shard_map/all_to_all | solution.py:42
  146.5 0.6 copy.102
  147.1 3.5 %all-to-all-start.5 = ((f32[16,2,1,1,128]{4,3,2,1,0:T(1,128)}), f32[16,2,1,1,128]{4,3,2,1,0:T(1,128)S(1)}, u32[]{:S(2)}, u32[]{:S(2)}) async-start(f32[16,2,1,1,128]{4,3,2,1,0:T(1,128)} %copy.102), calls=%async_computation.5 | async-start | bytes 32768 | tf_op jit(solution)/shard_map/all_to_all | solution.py:42
  150.6 0.1 squeeze.81
  150.7 6.3 %all-to-all-done.5 = f32[16,2,1,1,128]{4,3,2,1,0:T(1,128)S(1)} async-done(((f32[16,2,1,1,128]{4,3,2,1,0:T(1,128)}), f32[16,2,1,1,128]{4,3,2,1,0:T(1,128)S(1)}, u32[]{:S(2)}, u32[]{:S(2)}) %all-to-all-start.5) | async-done | bytes 16416 | tf_op jit(solution)/shard_map/all_to_all | solution.py:42
  157.0 7.6 %while.47 = (s32[]{:T(128)}, f32[2,512]{1,0:T(2,128)S(1)}, bf16[2,512,256]{2,1,0:T(8,128)(2,1)S(1)}, bf16[4096,256]{1,0:T(8,128)(2,1)}, f32[4096]{0:T(1024)S(1)}...) while((s32[]{:T(128)}, f32[2,512]{1,0:T(2,128)S(1)}, ...), condition=%wide.region_10.12_spmd.clone, body=%wide.region_8.11_spmd.clone.sunk | while | flops 1082134528 | bytes 2396269 | solution.py:113
  157.0 0.7 compare_reduce_fusion.6
  157.7 3.0 %select_reduce_fusion.10 = f32[512]{0:T(512)S(1)} fusion(bf16[4096,256]{1,0:T(8,128)(2,1)} %get-tuple-element.482, f32[4096]{0:T(1024)S(1)} %get-tuple-element.483, pred[4096]{0:T(1024)(128)(4,1)S(1)} %compare_reduce_fusion.6, bf16[2,512,256]{2,1,0:T(8,128)(2,1)S(1)} %get-tuple-element.481, s32[]{:T(128)} %get-tuple-element.470), kind=kOutput, calls=%fused_computation.4.clone.1 | convolution fusion | flops 1082129920 | bytes 2381828 | tf_op jit(solution)/shard_map/while/body/eval_jaxpr/while/body/eval_jaxpr/qd,kd->qk/dot_general | solution.py:104
  160.8 0.7 compare_reduce_fusion.6
  161.5 3.0 %select_reduce_fusion.10 = f32[512]{0:T(512)S(1)} fusion(bf16[4096,256]{1,0:T(8,128)(2,1)} %get-tuple-element.482, f32[4096]{0:T(1024)S(1)} %get-tuple-element.483, pred[4096]{0:T(1024)(128)(4,1)S(1)} %compare_reduce_fusion.6, bf16[2,512,256]{2,1,0:T(8,128)(2,1)S(1)} %get-tuple-element.481, s32[]{:T(128)} %get-tuple-element.470), kind=kOutput, calls=%fused_computation.4.clone.1 | convolution fusion | flops 1082129920 | bytes 2381828 | tf_op jit(solution)/shard_map/while/body/eval_jaxpr/while/body/eval_jaxpr/qd,kd->qk/dot_general | solution.py:104
  164.6 0.1 reshape.252
  164.7 1.4 compare_select_fusion
  166.0 4.9 %all-to-all-start.2 = ((f32[32,1,32]{2,1,0:T(1,128)}), f32[32,1,32]{2,1,0:T(1,128)S(1)}, u32[]{:S(2)}, u32[]{:S(2)}) async-start(f32[32,1,32]{2,1,0:T(1,128)} %get-tuple-element.313), calls=%async_computation.2 | async-start | bytes 32768 | tf_op jit(solution)/shard_map/all_to_all | solution.py:180
  171.0 7.1 %all-to-all-done.2 = f32[32,1,32]{2,1,0:T(1,128)S(1)} async-done(((f32[32,1,32]{2,1,0:T(1,128)}), f32[32,1,32]{2,1,0:T(1,128)S(1)}, u32[]{:S(2)}, u32[]{:S(2)}) %all-to-all-start.2) | async-done | bytes 4128 | tf_op jit(solution)/shard_map/all_to_all | solution.py:180
  178.0 4.2 %all-to-all-start.6 = ((f32[32,1,32]{2,1,0:T(1,128)}), f32[32,1,32]{2,1,0:T(1,128)S(1)}, u32[]{:S(2)}, u32[]{:S(2)}) async-start(f32[32,1,32]{2,1,0:T(1,128)} %get-tuple-element.312), calls=%async_computation.6 | async-start | bytes 32768 | tf_op jit(solution)/shard_map/all_to_all | solution.py:181
  182.2 0.7 add_select_fusion
  182.9 0.5 broadcast.201
  183.4 0.7 reduce.12
  184.1 0.7 reshape_transpose_reshape.10
  184.7 4.5 %all-to-all-done.6 = f32[32,1,32]{2,1,0:T(1,128)S(1)} async-done(((f32[32,1,32]{2,1,0:T(1,128)}), f32[32,1,32]{2,1,0:T(1,128)S(1)}, u32[]{:S(2)}, u32[]{:S(2)}) %all-to-all-start.6) | async-done | bytes 4128 | tf_op jit(solution)/shard_map/all_to_all | solution.py:181
  189.3 0.7 reduce.13
  190.0 0.7 reshape_transpose_reshape.11
  (31 shorter events, 0.5 us)
Async XLA Ops:
  0.6 8.6 %copy-start = (s32[8,2]{0,1:T(2,128)S(1)}, s32[8,2]{0,1:T(2,128)}, u32[]{:S(2)}) copy-start(s32[8,2]{0,1:T(2,128)} %param.10) | copy-start | bytes 196
  4.4 53.6 %all-to-all-start = ((bf16[4,16,128,256]{3,2,1,0:T(8,128)(2,1)}), bf16[4,16,128,256]{3,2,1,0:T(8,128)(2,1)}, u32[]{:S(2)}, u32[]{:S(2)}) async-start(bf16[4,16,128,256]{3,2,1,0:T(8,128)(2,1)} %stack.2), calls=%async_computation | async-start | bytes 8388608 | tf_op jit(solution)/shard_map/all_to_all | solution.py:198
  60.8 15.0 %copy-start.1 = (s32[64]{0:T(128)S(1)}, s32[64]{0:T(128)}, u32[]{:S(2)}) copy-start(s32[64]{0:T(128)} %param.11) | copy-start | bytes 772
  65.7 43.9 %all-to-all-start.1 = ((bf16[32,1,160,256]{3,2,1,0:T(8,128)(2,1)}), bf16[32,1,160,256]{3,2,1,0:T(8,128)(2,1)S(1)}, u32[]{:S(2)}, u32[]{:S(2)}) async-start(bf16[32,1,160,256]{3,2,1,0:T(8,128)(2,1)} %pad_maximum_fusion), calls=%async_computation.1 | async-start | bytes 5242880 | tf_op jit(solution)/shard_map/all_to_all | solution.py:16
  147.1 9.9 %all-to-all-start.5 = ((f32[16,2,1,1,128]{4,3,2,1,0:T(1,128)}), f32[16,2,1,1,128]{4,3,2,1,0:T(1,128)S(1)}, u32[]{:S(2)}, u32[]{:S(2)}) async-start(f32[16,2,1,1,128]{4,3,2,1,0:T(1,128)} %copy.102), calls=%async_computation.5 | async-start | bytes 32768 | tf_op jit(solution)/shard_map/all_to_all | solution.py:42
  166.0 12.0 %all-to-all-start.2 = ((f32[32,1,32]{2,1,0:T(1,128)}), f32[32,1,32]{2,1,0:T(1,128)S(1)}, u32[]{:S(2)}, u32[]{:S(2)}) async-start(f32[32,1,32]{2,1,0:T(1,128)} %get-tuple-element.313), calls=%async_computation.2 | async-start | bytes 32768 | tf_op jit(solution)/shard_map/all_to_all | solution.py:180
  178.0 11.2 %all-to-all-start.6 = ((f32[32,1,32]{2,1,0:T(1,128)}), f32[32,1,32]{2,1,0:T(1,128)S(1)}, u32[]{:S(2)}, u32[]{:S(2)}) async-start(f32[32,1,32]{2,1,0:T(1,128)} %get-tuple-element.312), calls=%async_computation.6 | async-start | bytes 32768 | tf_op jit(solution)/shard_map/all_to_all | solution.py:181
